TPU v7x, 32 devices: a whole 2x2x4 slice. The times are simulated.
32 devices in a mesh: sub: 2 (over y), row: 4 (over x, core), col: 4 (over z).
Axes of the slice: x: 2, y: 2, z: 4, core: 2. Of those that a mesh axis runs over, the one named last changes fastest.
Arguments:
- factor_window: bfloat16 [2, 8192, 1024], P('sub', ('row', 'col'))
- right_sides: bfloat16 [2, 8192, 2048], P('sub', 'row', 'col'), may hold values from -1.1953125 to 1.1953125
- first_block: int32 [2, 8], P('sub'), may hold values from 0 to 4
- tile_map: int32 [2, 8], P('sub'), may hold values from 0 to 15, as said below
- interface_block: float32 [4096, 4096], P(('sub', 'row'), 'col'), may hold values from -6 to 6
Outputs:
- updated_sides: bfloat16 [2, 8192, 2048], P('sub', 'row', 'col')
- schur_global: float32 [4096, 4096], P(('sub', 'row'), 'col')
Inputs may be any that keep to these rules, and one draw needn't show every extreme that they name: `tile_map`: the 8 entries of a subdomain are different global tiles.
All inputs are finite; a program needn't handle non-finite values.
Results may differ from a plain program's by a relative error of at most 0.0075.
Values may be sent and summed in bfloat16 or wider, within the bound.
A program may use at most 64 MiB of HBM per device.

v0:
```python
import jax
import jax.numpy as jnp
from jax import lax
from jax.sharding import PartitionSpec as P

PANEL = 256
BLOCK = 256
STEPS = 4
GTILES = 16


def spread_2(value, axis, source):
    kept = jnp.where(lax.axis_index(axis) == source, value, 0).astype(value.dtype)
    return lax.psum(kept, axis)


def spread_tiles(columns, tile_map, block_count):
    onehot = (tile_map[0][:, None] == jnp.arange(GTILES, dtype=jnp.int32)[None, :]).astype(
        jnp.bfloat16
    )
    height = columns.shape[0]
    spread = jnp.einsum(
        "qbj,bg->qgj",
        columns.reshape(height, block_count, BLOCK),
        onehot,
        preferred_element_type=jnp.float32,
    )
    return spread.reshape(height, GTILES * BLOCK).astype(jnp.bfloat16)


def local(factor_window, right_sides, first_block, tile_map, interface_block):
    row_count = lax.axis_size("row")
    row_pos = lax.axis_index("row")
    col_pos = lax.axis_index("col")
    local_factor = factor_window[0]
    local_sides = right_sides[0]
    block_rows = local_sides.shape[0]
    block_cols = local_sides.shape[1]
    block_count = first_block.shape[1]
    row_global = row_pos * block_rows + jnp.arange(block_rows, dtype=jnp.int32)
    col_global = col_pos * block_cols + jnp.arange(block_cols, dtype=jnp.int32)
    col_block = col_global // BLOCK
    block_ids = jnp.arange(block_count, dtype=jnp.int32)
    first_col = jnp.sum(
        jnp.where(col_block[:, None] == block_ids[None, :], first_block[0][None, :], 0), axis=1
    )
    live = (row_global // PANEL)[:, None] >= first_col[None, :]
    current = jnp.where(live, local_sides.astype(jnp.float32), jnp.float32(0.0))
    is_root = row_pos == 0
    factor_rows = lax.all_gather(local_factor, "col", axis=0, tiled=True)
    pieces = []
    for panel in range(STEPS):
        offset = panel * PANEL
        panel_cols = factor_rows[:, offset : offset + PANEL]
        diag_block = panel_cols[offset : offset + PANEL].astype(jnp.float32)
        diag_block = jnp.where(is_root, diag_block, jnp.eye(PANEL, dtype=jnp.float32))
        solved = jax.scipy.linalg.solve_triangular(
            diag_block, current[offset : offset + PANEL], lower=True
        ).astype(jnp.bfloat16)
        solved = spread_2(solved, "row", 0)
        update = jnp.dot(panel_cols, solved, preferred_element_type=jnp.float32)
        current = jnp.where((row_global >= offset + PANEL)[:, None], current - update, current)
        placed = jnp.where(is_root, solved.astype(jnp.float32), current[offset : offset + PANEL])
        current = current.at[offset : offset + PANEL].set(placed)
        pieces.append(solved)
    updated_sides = current.astype(jnp.bfloat16)[None]
    stacked = jnp.concatenate(pieces, axis=0)
    out_cols = interface_block.shape[1]
    share = stacked.shape[0] // row_count
    my_share = lax.dynamic_slice_in_dim(stacked, row_pos * share, share, 0)
    all_columns = lax.all_gather(my_share, "col", axis=1, tiled=True)
    spread = spread_tiles(all_columns, tile_map, block_count)
    my_columns = lax.dynamic_slice_in_dim(spread, col_pos * out_cols, out_cols, 1)
    summed = lax.psum_scatter(
        lax.dot_general(
            spread, my_columns, (((0,), (0,)), ((), ())), preferred_element_type=jnp.float32
        ).astype(jnp.bfloat16),
        ("sub", "row"),
        scatter_dimension=0,
        tiled=True,
    ).astype(jnp.float32)
    schur_global = interface_block - summed
    return (updated_sides, schur_global)


def solution(mesh):
    return jax.shard_map(
        local,
        mesh=mesh,
        in_specs=(
            P("sub", ("row", "col"), None),
            P("sub", "row", "col"),
            P("sub", None),
            P("sub", None),
            P(("sub", "row"), "col"),
        ),
        out_specs=(P("sub", "row", "col"), P(("sub", "row"), "col")),
        check_vma=False,
    )
```

profile of v0, /device:TPU:0, one launch (start us, length us, event | category | flops | bytes accessed | tf_op | source)
XLA Modules:
  0.0 394.8 jit_solution(10873900418680429173)
XLA Ops:
  7.2 0.7 all-gather.6.cloned.1.call-update
  8.0 0.7 select_reduce_fusion
  8.8 3.5 convert_select_fusion
  12.3 80.8 %all-gather.6.cloned.1.call-done = bf16[1,2048,1024]{2,1,0:T(8,128)(2,1)} async-done(((bf16[1,512,1024]{2,1,0:T(8,128)(2,1)}), bf16[1,2048,1024]{2,1,0:T(8,128)(2,1)}) %all-gather.6.cloned.1.call-update) | async-done | bytes 4194320 | tf_op jit(solution)/shard_map/all_gather | solution.py:50
  93.0 1.2 fusion.16
  94.3 3.8 while.12
  94.9 1.3 bitcast_dynamic-update-slice_fusion.8
  96.8 1.3 bitcast_dynamic-update-slice_fusion.8
  98.1 19.7 %custom-call.6 = f32[2,128,128]{1,2,0:T(8,128)S(1)} custom-call(f32[2,128,128]{2,1,0:T(8,128)S(1)} %get-tuple-element.77), custom_call_target="InvertDiagBlocksLowerTriangular" | custom-call | tf_op jit(solution)/shard_map/jit(_solve_triangular)/triangular_solve | solution.py:57
  117.8 1.4 fusion.26
  119.2 1.3 convolution_subtract_fusion.3
  120.9 0.7 fusion.12
  121.7 4.0 %while.13 = (s32[]{:T(128)}, f32[256,256]{1,0:T(8,128)S(1)}, s32[2,2]{1,0:T(2,128)S(1)}, f32[2,128,128]{2,1,0:T(8,128)S(1)}, s32[]{:T(128)}) while((s32[]{:T(128)}, f32[256,256]{1,0:T(8,128)S(1)}, s32[2,2]{1,0:T(2,128)S(1)}, f32[2,128,128]{2,1,0:T(8,128)S(1)}, s32[]{:T(128)}) %tuple.113), condition=%wide.while_cond.4.clone, body=%wide.while_body.4.clone.sunk | while | flops 2 | bytes 131181 | solution.py:57
  121.8 0.7 fusion.73
  122.4 1.3 bitcast_dynamic-update-slice_fusion.9
  123.8 0.7 fusion.73
  124.5 1.3 bitcast_dynamic-update-slice_fusion.9
  125.8 19.7 %custom-call.7 = f32[2,128,128]{1,2,0:T(8,128)S(1)} custom-call(f32[2,128,128]{2,1,0:T(8,128)S(1)} %get-tuple-element.78), custom_call_target="InvertDiagBlocksLowerTriangular" | custom-call | tf_op jit(solution)/shard_map/jit(_solve_triangular)/triangular_solve | solution.py:57
  145.5 7.4 %all-reduce.5.cloned.1.call-done = bf16[256,512]{1,0:T(8,128)(2,1)} async-done(((bf16[256,512]{1,0:T(8,128)(2,1)}), bf16[256,512]{1,0:T(8,128)(2,1)}) %all-reduce.5.cloned.1.call-update) | async-done | bytes 262160 | tf_op jit(solution)/shard_map/psum | solution.py:14
  152.9 3.4 subtract_select_fusion.3
  156.8 1.6 copy-done.2
  159.2 0.7 fusion.11
  160.2 4.0 %while.14 = (s32[]{:T(128)}, f32[256,256]{1,0:T(8,128)S(1)}, s32[2,2]{1,0:T(2,128)S(1)}, f32[2,128,128]{2,1,0:T(8,128)S(1)}, s32[]{:T(128)}) while((s32[]{:T(128)}, f32[256,256]{1,0:T(8,128)S(1)}, s32[2,2]{1,0:T(2,128)S(1)}, f32[2,128,128]{2,1,0:T(8,128)S(1)}, s32[]{:T(128)}) %tuple.114), condition=%wide.while_cond.4.clone.1, body=%wide.while_body.4.clone.1.sunk | while | flops 2 | bytes 131181 | solution.py:57
  160.8 1.4 bitcast_dynamic-update-slice_fusion.10
  162.8 1.4 bitcast_dynamic-update-slice_fusion.10
  164.2 19.7 %custom-call.8 = f32[2,128,128]{1,2,0:T(8,128)S(1)} custom-call(f32[2,128,128]{2,1,0:T(8,128)S(1)} %get-tuple-element.79), custom_call_target="InvertDiagBlocksLowerTriangular" | custom-call | tf_op jit(solution)/shard_map/jit(_solve_triangular)/triangular_solve | solution.py:57
  183.9 8.8 %all-reduce.7.cloned.1.call-done = bf16[256,512]{1,0:T(8,128)(2,1)} async-done(((bf16[256,512]{1,0:T(8,128)(2,1)}), bf16[256,512]{1,0:T(8,128)(2,1)}) %all-reduce.7.cloned.1.call-update) | async-done | bytes 262160 | tf_op jit(solution)/shard_map/psum | solution.py:14
  192.7 3.4 subtract_select_fusion.2
  196.7 1.6 copy-done.1
  199.0 0.7 fusion.10
  199.9 3.8 while.15
  200.5 1.3 bitcast_dynamic-update-slice_fusion.11
  202.4 1.3 bitcast_dynamic-update-slice_fusion.11
  203.7 19.7 %custom-call.9 = f32[2,128,128]{1,2,0:T(8,128)S(1)} custom-call(f32[2,128,128]{2,1,0:T(8,128)S(1)} %get-tuple-element.80), custom_call_target="InvertDiagBlocksLowerTriangular" | custom-call | tf_op jit(solution)/shard_map/jit(_solve_triangular)/triangular_solve | solution.py:57
  223.4 9.2 %all-reduce.9.cloned.1.call-done = bf16[256,512]{1,0:T(8,128)(2,1)} async-done(((bf16[256,512]{1,0:T(8,128)(2,1)}), bf16[256,512]{1,0:T(8,128)(2,1)}) %all-reduce.9.cloned.1.call-update) | async-done | bytes 262160 | tf_op jit(solution)/shard_map/psum | solution.py:14
  232.5 3.4 subtract_select_fusion.1
  236.5 1.6 copy-done
  238.8 0.7 fusion.9
  239.7 32.3 %all-reduce.11.cloned.1.call-done = bf16[256,512]{1,0:T(8,128)(2,1)} async-done(((bf16[256,512]{1,0:T(8,128)(2,1)}), bf16[256,512]{1,0:T(8,128)(2,1)}) %all-reduce.11.cloned.1.call-update) | async-done | bytes 262160 | tf_op jit(solution)/shard_map/psum | solution.py:14
  272.0 3.4 subtract_select_fusion
  275.4 1.6 fusion.19
  277.2 27.9 %all-gather.4.cloned.1.call-done = bf16[256,2048]{1,0:T(8,128)(2,1)} async-done(((bf16[256,512]{1,0:T(8,128)(2,1)}), bf16[256,2048]{1,0:T(8,128)(2,1)}) %all-gather.4.cloned.1.call-update) | async-done | bytes 1048592 | tf_op jit(solution)/shard_map/all_gather | solution.py:71
  305.1 1.5 copy.19
  306.7 0.8 convolution_convert_fusion.1
  307.5 0.9 copy.20
  308.4 5.6 %convolution_convert_fusion = bf16[4096,1024]{1,0:T(8,128)(2,1)} fusion(bf16[256,4096]{1,0:T(8,128)(2,1)S(1)} %bitcast.105, s32[]{:T(128)S(6)} %select_n.126), kind=kOutput, calls=%fused_computation.8 | convolution fusion | flops 2151677952 | bytes 11010052 | tf_op jit(solution)/shard_map/dot_general | solution.py:75
  314.1 71.0 %reduce-scatter.2.cloned.1.call-done = bf16[512,1024]{1,0:T(8,128)(2,1)} async-done(((bf16[4096,1024]{1,0:T(8,128)(2,1)}), bf16[512,1024]{1,0:T(8,128)(2,1)}) %reduce-scatter.2.cloned.1.call-update) | async-done | bytes 1048592 | tf_op jit(solution)/shard_map/reduce_scatter | solution.py:74
  385.1 2.8 convert_subtract_fusion
  (71 shorter events, 9.0 us)
Async XLA Ops:
  7.2 85.9 %all-gather.6.cloned.1.call-start = ((), (), s32[]{:S(2)}) async-start(), calls=%async_computation.7 | async-start | bytes 5242880 | tf_op jit(solution)/shard_map/all_gather | solution.py:50
  7.9 145.0 %all-reduce.5.cloned.1.call-start = ((), (), s32[]{:S(2)}) async-start(), calls=%async_computation.1 | async-start | bytes 524288 | tf_op jit(solution)/shard_map/psum | solution.py:14
  12.3 140.6 %copy-start.6 = (bf16[1,2048,512]{2,1,0:T(8,128)(2,1)S(1)}, bf16[1,2048,512]{2,1,0:T(8,128)(2,1)}, u32[]{:S(2)}) copy-start(bf16[1,2048,512]{2,1,0:T(8,128)(2,1)} %param.16) | copy-start | bytes 6291460
  121.7 71.0 %all-reduce.7.cloned.1.call-start = ((), (), s32[]{:S(2)}) async-start(), calls=%async_computation.2 | async-start | bytes 524288 | tf_op jit(solution)/shard_map/psum | solution.py:14
  152.9 3.4 copy-start.8
  156.4 2.0 copy-start.2
  160.0 72.6 %all-reduce.9.cloned.1.call-start = ((), (), s32[]{:S(2)}) async-start(), calls=%async_computation.3 | async-start | bytes 524288 | tf_op jit(solution)/shard_map/psum | solution.py:14
  192.7 3.4 copy-start.4
  196.2 2.0 copy-start.1
  199.8 72.2 %all-reduce.11.cloned.1.call-start = ((), (), s32[]{:S(2)}) async-start(), calls=%async_computation.4 | async-start | bytes 524288 | tf_op jit(solution)/shard_map/psum | solution.py:14
  232.5 3.4 copy-start.5
  236.0 2.0 copy-start
  239.6 65.5 %all-gather.4.cloned.1.call-start = ((), (), s32[]{:S(2)}) async-start(), calls=%async_computation.5 | async-start | bytes 1310720 | tf_op jit(solution)/shard_map/all_gather | solution.py:71
  239.7 67.0 %copy-start.10 = (s32[1,8]{1,0:T(1,128)S(1)}, s32[1,8]{1,0:T(1,128)}, u32[]{:S(2)}) copy-start(s32[1,8]{1,0:T(1,128)} %param.18) | copy-start | bytes 100
  272.0 3.4 copy-start.9
  276.9 31.5 %copy-start.3 = (bf16[2048,512]{1,0:T(8,128)(2,1)}, bf16[2048,512]{1,0:T(8,128)(2,1)S(1)}, u32[]{:S(2)}) copy-start(bf16[2048,512]{1,0:T(8,128)(2,1)S(1)} %get-tuple-element.126) | copy-start | bytes 6291460
  277.0 108.2 %reduce-scatter.2.cloned.1.call-start = ((), (), s32[]{:S(2)}) async-start(), calls=%async_computation.6 | async-start | bytes 9437184 | tf_op jit(solution)/shard_map/reduce_scatter | solution.py:74
  314.1 71.1 %copy-start.7 = (f32[512,1024]{1,0:T(8,128)S(1)}, f32[512,1024]{1,0:T(8,128)}, u32[]{:S(2)}) copy-start(f32[512,1024]{1,0:T(8,128)} %param.19) | copy-start | bytes 6291460
Sparse Core Ops, SparseCore 0:
  9.5 83.4 all-gather.5
  121.8 31.0 all-reduce.4
  160.1 32.5 all-reduce.6
  199.9 32.5 all-reduce.8
  239.7 32.2 all-reduce.10
  277.1 27.9 all-gather.3
  314.2 70.8 reduce-scatter.1
where the time goes:
time: 395 us
  waiting for transfers between devices  238 us (60%)
  other arithmetic  92 us (23%)
  matrix products  26.7 us (7%)
  local copies, waits for them, and re-layouts  22.7 us (6%)
  between operations  14.5 us (4%)
    all_gather x1, waiting for transfers between devices, local(): factor_rows = lax.all_gather(local_factor, 'col', axis=0, tiled=True)  80.8 us
    another operation x6, other arithmetic, local(): jax.scipy.linalg.solve_triangular(diag_block, current[offset:offset + PAN...  79.9 us
    reduce_scatter x1, waiting for transfers between devices, local(): lax.psum_scatter(lax.dot_general(spread, my_columns, (((0,), (0,)), ((),...  71 us
    psum x4, waiting for transfers between devices, spread_2(): return lax.psum(kept, axis)  57.7 us
    all_gather x1, waiting for transfers between devices, local(): all_columns = lax.all_gather(my_share, 'col', axis=1, tiled=True)  27.9 us
    another operation x29, local copies, waits for them, and re-layouts, local(): jax.scipy.linalg.solve_triangular(diag_block, current[offset:offset + PAN...  15.5 us
    dot_general x4, matrix products, local(): update = jnp.dot(panel_cols, solved, preferred_element_type=jnp.float32)  13.4 us
  transfers between devices with their start and end apart: 7, of which 7 were waited for; matrix products, arithmetic and copies ran while one was open for 19% of the time, Pallas kernels for 0%

commit v1 on v0

--- a/solution.py
+++ b/solution.py
@@ -11,7 +11,8 @@
 
 def spread_2(value, axis, source):
     kept = jnp.where(lax.axis_index(axis) == source, value, 0).astype(value.dtype)
-    return lax.psum(kept, axis)
+    direct_the_shards = lambda t0, device_axis: jnp.sum(lax.all_gather(t0, device_axis), 0)
+    return direct_the_shards(kept, axis)
 
 
 def spread_tiles(columns, tile_map, block_count):

time: 395 us -> 358 us (0.906)
  waiting for transfers between devices: 238 us -> 196 us
  other arithmetic: 92 us -> 97.8 us
    psum x4 -> x0, waiting for transfers between devices: 57.7 us -> none  [spread_2(): return lax.psum(kept, axis)]
    all_gather x0 -> x4, waiting for transfers between devices: none -> 15.4 us  [spread_2(): lax.all_gather(t0, device_axis)]
    reduce_sum x0 -> x4, other arithmetic: none -> 5.82 us  [spread_2(): jnp.sum(lax.all_gather(t0, device_axis), 0)]
  transfers between devices with their start and end apart: 7 -> 7, of which waited for: 7 -> 4; matrix products, arithmetic and copies ran while one was open for 19% -> 21% of each run, Pallas kernels for 0% -> 0%
where the time goes in v1:
time: 358 us
  waiting for transfers between devices  196 us (55%)
  other arithmetic  97.8 us (27%)
  matrix products  26.2 us (7%)
  local copies, waits for them, and re-layouts  22.3 us (6%)
  between operations  14.5 us (4%)
    all_gather x1, waiting for transfers between devices, local(): factor_rows = lax.all_gather(local_factor, 'col', axis=0, tiled=True)  80.8 us
    another operation x6, other arithmetic, local(): jax.scipy.linalg.solve_triangular(diag_block, current[offset:offset + PAN...  79.9 us
    reduce_scatter x1, waiting for transfers between devices, local(): lax.psum_scatter(lax.dot_general(spread, my_columns, (((0,), (0,)), ((),...  71 us
    all_gather x1, waiting for transfers between devices, local(): all_columns = lax.all_gather(my_share, 'col', axis=1, tiled=True)  27.9 us
    all_gather x4, waiting for transfers between devices, spread_2(): lax.all_gather(t0, device_axis)  15.4 us
    another operation x29, local copies, waits for them, and re-layouts, local(): jax.scipy.linalg.solve_triangular(diag_block, current[offset:offset + PAN...  15.2 us
    dot_general x4, matrix products, local(): update = jnp.dot(panel_cols, solved, preferred_element_type=jnp.float32)  13 us
  transfers between devices with their start and end apart: 7, of which 4 were waited for; matrix products, arithmetic and copies ran while one was open for 21% of the time, Pallas kernels for 0%

profile of v1, /device:TPU:0, one launch (start us, length us, event | category | flops | bytes accessed | tf_op | source)
XLA Modules:
  0.0 357.5 jit_solution(5562600036931569421)
XLA Ops:
  7.2 0.7 all-gather.14.cloned.1.call-update
  8.0 0.7 select_reduce_fusion
  8.7 3.5 convert_select_fusion
  12.2 80.8 %all-gather.14.cloned.1.call-done = bf16[1,2048,1024]{2,1,0:T(8,128)(2,1)} async-done(((bf16[1,512,1024]{2,1,0:T(8,128)(2,1)}), bf16[1,2048,1024]{2,1,0:T(8,128)(2,1)}) %all-gather.14.cloned.1.call-update) | async-done | bytes 4194320 | tf_op jit(solution)/shard_map/all_gather | solution.py:51
  93.0 1.2 fusion.16
  94.3 4.0 %while.12 = (s32[]{:T(128)}, f32[256,256]{1,0:T(8,128)S(1)}, s32[2,2]{1,0:T(2,128)S(1)}, f32[2,128,128]{2,1,0:T(8,128)S(1)}, s32[]{:T(128)}) while((s32[]{:T(128)}, f32[256,256]{1,0:T(8,128)S(1)}, s32[2,2]{1,0:T(2,128)S(1)}, f32[2,128,128]{2,1,0:T(8,128)S(1)}, s32[]{:T(128)}) %tuple.87), condition=%wide.while_cond.4, body=%wide.while_body.4.sunk | while | flops 2 | bytes 131181 | solution.py:58
  94.9 1.4 bitcast_dynamic-update-slice_fusion.8
  96.9 1.4 bitcast_dynamic-update-slice_fusion.8
  98.3 19.7 %custom-call.6 = f32[2,128,128]{1,2,0:T(8,128)S(1)} custom-call(f32[2,128,128]{2,1,0:T(8,128)S(1)} %get-tuple-element.77), custom_call_target="InvertDiagBlocksLowerTriangular" | custom-call | tf_op jit(solution)/shard_map/jit(_solve_triangular)/triangular_solve | solution.py:58
  118.0 1.4 fusion.26
  119.4 1.3 convolution_subtract_fusion.3
  121.1 0.7 fusion.12
  122.0 3.8 %while.13 = (s32[]{:T(128)}, f32[256,256]{1,0:T(8,128)S(1)}, s32[2,2]{1,0:T(2,128)S(1)}, f32[2,128,128]{2,1,0:T(8,128)S(1)}, s32[]{:T(128)}) while((s32[]{:T(128)}, f32[256,256]{1,0:T(8,128)S(1)}, s32[2,2]{1,0:T(2,128)S(1)}, f32[2,128,128]{2,1,0:T(8,128)S(1)}, s32[]{:T(128)}) %tuple.113), condition=%wide.while_cond.4.clone, body=%wide.while_body.4.clone.sunk | while | flops 2 | bytes 131181 | solution.py:58
  122.6 1.3 bitcast_dynamic-update-slice_fusion.9
  124.5 1.3 bitcast_dynamic-update-slice_fusion.9
  125.7 19.7 %custom-call.7 = f32[2,128,128]{1,2,0:T(8,128)S(1)} custom-call(f32[2,128,128]{2,1,0:T(8,128)S(1)} %get-tuple-element.78), custom_call_target="InvertDiagBlocksLowerTriangular" | custom-call | tf_op jit(solution)/shard_map/jit(_solve_triangular)/triangular_solve | solution.py:58
  145.5 1.5 reduce_sum.58
  146.9 3.3 subtract_select_fusion.3
  150.8 1.5 copy-done.2
  153.1 0.7 fusion.11
  154.2 3.8 %while.14 = (s32[]{:T(128)}, f32[256,256]{1,0:T(8,128)S(1)}, s32[2,2]{1,0:T(2,128)S(1)}, f32[2,128,128]{2,1,0:T(8,128)S(1)}, s32[]{:T(128)}) while((s32[]{:T(128)}, f32[256,256]{1,0:T(8,128)S(1)}, s32[2,2]{1,0:T(2,128)S(1)}, f32[2,128,128]{2,1,0:T(8,128)S(1)}, s32[]{:T(128)}) %tuple.114), condition=%wide.while_cond.4.clone.1, body=%wide.while_body.4.clone.1.sunk | while | flops 2 | bytes 131181 | solution.py:58
  154.8 1.3 bitcast_dynamic-update-slice_fusion.10
  156.1 0.6 fusion.74
  156.7 1.3 bitcast_dynamic-update-slice_fusion.10
  158.0 19.7 %custom-call.8 = f32[2,128,128]{1,2,0:T(8,128)S(1)} custom-call(f32[2,128,128]{2,1,0:T(8,128)S(1)} %get-tuple-element.79), custom_call_target="InvertDiagBlocksLowerTriangular" | custom-call | tf_op jit(solution)/shard_map/jit(_solve_triangular)/triangular_solve | solution.py:58
  177.7 1.5 reduce_sum.59
  179.1 3.2 subtract_select_fusion.2
  183.0 1.5 copy-done.1
  185.3 0.7 fusion.10
  186.1 3.8 %while.15 = (s32[]{:T(128)}, f32[256,256]{1,0:T(8,128)S(1)}, s32[2,2]{1,0:T(2,128)S(1)}, f32[2,128,128]{2,1,0:T(8,128)S(1)}, s32[]{:T(128)}) while((s32[]{:T(128)}, f32[256,256]{1,0:T(8,128)S(1)}, s32[2,2]{1,0:T(2,128)S(1)}, f32[2,128,128]{2,1,0:T(8,128)S(1)}, s32[]{:T(128)}) %tuple.115), condition=%wide.while_cond.4.clone.2, body=%wide.while_body.4.clone.2.sunk | while | flops 2 | bytes 131181 | solution.py:58
  186.8 1.3 bitcast_dynamic-update-slice_fusion.11
  188.7 1.3 bitcast_dynamic-update-slice_fusion.11
  189.9 19.7 %custom-call.9 = f32[2,128,128]{1,2,0:T(8,128)S(1)} custom-call(f32[2,128,128]{2,1,0:T(8,128)S(1)} %get-tuple-element.80), custom_call_target="InvertDiagBlocksLowerTriangular" | custom-call | tf_op jit(solution)/shard_map/jit(_solve_triangular)/triangular_solve | solution.py:58
  209.7 1.5 reduce_sum.60
  211.1 3.2 subtract_select_fusion.1
  214.9 1.5 copy-done
  217.3 0.7 fusion.9
  218.1 15.3 %all-gather.22.cloned.1.call-done = bf16[1024,512]{1,0:T(8,128)(2,1)} async-done(((bf16[256,512]{1,0:T(8,128)(2,1)}), bf16[1024,512]{1,0:T(8,128)(2,1)}) %all-gather.22.cloned.1.call-update) | async-done | bytes 1048592 | tf_op jit(solution)/shard_map/all_gather | solution.py:14
  233.4 1.5 reduce_sum.61
  234.9 3.2 subtract_select_fusion
  238.1 1.6 fusion.19
  240.0 27.9 %all-gather.12.cloned.1.call-done = bf16[256,2048]{1,0:T(8,128)(2,1)} async-done(((bf16[256,512]{1,0:T(8,128)(2,1)}), bf16[256,2048]{1,0:T(8,128)(2,1)}) %all-gather.12.cloned.1.call-update) | async-done | bytes 1048592 | tf_op jit(solution)/shard_map/all_gather | solution.py:72
  267.9 1.5 copy.19
  269.4 0.8 convolution_convert_fusion.1
  270.2 0.9 copy.20
  271.2 5.6 %convolution_convert_fusion = bf16[4096,1024]{1,0:T(8,128)(2,1)} fusion(bf16[256,4096]{1,0:T(8,128)(2,1)S(1)} %bitcast.109, s32[]{:T(128)S(6)} %select_n.126), kind=kOutput, calls=%fused_computation.8 | convolution fusion | flops 2151677952 | bytes 11010052 | tf_op jit(solution)/shard_map/dot_general | solution.py:76
  276.8 71.0 %reduce-scatter.2.cloned.1.call-done = bf16[512,1024]{1,0:T(8,128)(2,1)} async-done(((bf16[4096,1024]{1,0:T(8,128)(2,1)}), bf16[512,1024]{1,0:T(8,128)(2,1)}) %reduce-scatter.2.cloned.1.call-update) | async-done | bytes 1048592 | tf_op jit(solution)/shard_map/reduce_scatter | solution.py:75
  347.9 2.8 convert_subtract_fusion
  (67 shorter events, 9.6 us)
Async XLA Ops:
  7.2 85.9 %all-gather.14.cloned.1.call-start = ((), (), s32[]{:S(2)}) async-start(), calls=%async_computation.3 | async-start | bytes 5242880 | tf_op jit(solution)/shard_map/all_gather | solution.py:51
  7.9 137.6 %all-gather.16.cloned.1.call-start = ((), (), s32[]{:S(2)}) async-start(), calls=%async_computation.4 | async-start | bytes 1310720 | tf_op jit(solution)/shard_map/all_gather | solution.py:14
  12.2 134.7 %copy-start.4 = (bf16[1,2048,512]{2,1,0:T(8,128)(2,1)S(1)}, bf16[1,2048,512]{2,1,0:T(8,128)(2,1)}, u32[]{:S(2)}) copy-start(bf16[1,2048,512]{2,1,0:T(8,128)(2,1)} %param.16) | copy-start | bytes 6291460
  121.9 55.8 %all-gather.18.cloned.1.call-start = ((), (), s32[]{:S(2)}) async-start(), calls=%async_computation.5 | async-start | bytes 1310720 | tf_op jit(solution)/shard_map/all_gather | solution.py:14
  150.3 2.0 copy-start.2
  153.9 55.8 %all-gather.20.cloned.1.call-start = ((), (), s32[]{:S(2)}) async-start(), calls=%async_computation.6 | async-start | bytes 1310720 | tf_op jit(solution)/shard_map/all_gather | solution.py:14
  182.5 2.0 copy-start.1
  186.1 47.3 %all-gather.22.cloned.1.call-start = ((), (), s32[]{:S(2)}) async-start(), calls=%async_computation.7 | async-start | bytes 1310720 | tf_op jit(solution)/shard_map/all_gather | solution.py:14
  214.5 2.0 copy-start
  218.0 49.8 %all-gather.12.cloned.1.call-start = ((), (), s32[]{:S(2)}) async-start(), calls=%async_computation.1 | async-start | bytes 1310720 | tf_op jit(solution)/shard_map/all_gather | solution.py:72
  234.9 34.5 %copy-start.6 = (s32[1,8]{1,0:T(1,128)S(1)}, s32[1,8]{1,0:T(1,128)}, u32[]{:S(2)}) copy-start(s32[1,8]{1,0:T(1,128)} %param.18) | copy-start | bytes 100
  239.7 31.5 %copy-start.3 = (bf16[2048,512]{1,0:T(8,128)(2,1)}, bf16[2048,512]{1,0:T(8,128)(2,1)S(1)}, u32[]{:S(2)}) copy-start(bf16[2048,512]{1,0:T(8,128)(2,1)S(1)} %get-tuple-element.126) | copy-start | bytes 6291460
  239.7 108.1 %reduce-scatter.2.cloned.1.call-start = ((), (), s32[]{:S(2)}) async-start(), calls=%async_computation.2 | async-start | bytes 9437184 | tf_op jit(solution)/shard_map/reduce_scatter | solution.py:75
  276.8 71.1 %copy-start.5 = (f32[512,1024]{1,0:T(8,128)S(1)}, f32[512,1024]{1,0:T(8,128)}, u32[]{:S(2)}) copy-start(f32[512,1024]{1,0:T(8,128)} %param.19) | copy-start | bytes 6291460
Sparse Core Ops, SparseCore 0:
  9.5 83.4 all-gather.13
  122.0 15.3 all-gather.15
  154.0 15.5 all-gather.17
  186.2 15.3 all-gather.19
  218.2 15.1 all-gather.21
  239.8 27.9 all-gather.11
  276.9 70.8 reduce-scatter.1
